TPU v7x, 256 devices: a whole 4x4x8 slice. The times are simulated.
256 devices in a mesh: outer: 16 (over z_lo, y), inner: 16 (over x, z_hi, core).
Axes of the slice: x: 4, y: 4, z: 8 (z_hi: 2, z_lo: 4; z = z_hi * 4 + z_lo), core: 2. Of those that a mesh axis runs over, the one named last changes fastest.
Arguments:
- stem_real: float32 [16, 16, 256, 512], P('outer', 'inner'), may hold values from -6 to 6
- stem_imag: float32 [16, 16, 256, 512], P('outer', 'inner'), may hold values from -6 to 6
- branch_real: float32 [4, 512, 512], replicated, may hold values from -0.1875 to 0.1875
- branch_imag: float32 [4, 512, 512], replicated, may hold values from -0.1875 to 0.1875
- orders: int32 [4, 512], replicated, may hold values from 0 to 511, each once within a row
Outputs:
- out_real: float32 [16, 16, 256, 512], P('outer', 'inner')
- out_imag: float32 [16, 16, 256, 512], P('outer', 'inner')
Inputs may be any that keep to these rules, and one draw needn't show every extreme that they name: Each row of orders holds every index of 0 to 511 once.
All inputs are finite; a program needn't handle non-finite values.
Results may differ from a plain program's by a relative error of at most 0.0001.
Values sent between devices are 32-bit elements; how exact they have to be, the bound alone decides.
No kernel may reach another device: no remote copies, remote signals or barrier semaphores. Data moves between devices by JAX's collectives and lax.ppermute only.
A program may use at most 64 MiB of HBM per device.

v0:
```python
import jax
import jax.numpy as jnp
from jax import lax
from jax.sharding import PartitionSpec as P

PRODUCTS = 4


def prepare(branch_real, branch_imag, order):
    width = branch_real.shape[0]
    places = lax.broadcasted_iota(jnp.int32, (width, width), 0)
    selector = (places == order[None, :]).astype(jnp.float32)
    moved_real = jnp.dot(
        selector, branch_real, precision=lax.Precision.HIGHEST, preferred_element_type=jnp.float32
    )
    moved_imag = jnp.dot(
        selector, branch_imag, precision=lax.Precision.HIGHEST, preferred_element_type=jnp.float32
    )
    return (moved_real, moved_imag, moved_real + moved_imag)


def product(plane_real, plane_imag, prepared):
    moved_real, moved_imag, moved_sum = prepared
    width = moved_real.shape[0]
    count = plane_real.size // width
    left_real = plane_real.reshape(count, width)
    left_imag = plane_imag.reshape(count, width)
    first = jnp.dot(
        left_real, moved_real, precision=lax.Precision.HIGHEST, preferred_element_type=jnp.float32
    )
    second = jnp.dot(
        left_imag, moved_imag, precision=lax.Precision.HIGHEST, preferred_element_type=jnp.float32
    )
    third = jnp.dot(
        left_real + left_imag,
        moved_sum,
        precision=lax.Precision.HIGHEST,
        preferred_element_type=jnp.float32,
    )
    return (
        (first - second).reshape(1, 1, count, width),
        (third - first - second).reshape(1, 1, count, width),
    )


def inner_step(plane_real, plane_imag, prepared):
    return product(
        lax.all_to_all(plane_real, "inner", split_axis=3, concat_axis=3, tiled=True),
        lax.all_to_all(plane_imag, "inner", split_axis=3, concat_axis=3, tiled=True),
        prepared,
    )


def outer_step(plane_real, plane_imag, prepared):
    return product(
        lax.all_to_all(plane_real, "outer", split_axis=3, concat_axis=3, tiled=True),
        lax.all_to_all(plane_imag, "outer", split_axis=3, concat_axis=3, tiled=True),
        prepared,
    )


def on_device(stem_real, stem_imag, branch_real, branch_imag, orders):
    tables = [
        prepare(branch_real[step], branch_imag[step], orders[step]) for step in range(PRODUCTS)
    ]
    plane_real, plane_imag = product(stem_real, stem_imag, tables[0])
    plane_real, plane_imag = inner_step(plane_real, plane_imag, tables[1])
    plane_real, plane_imag = outer_step(plane_real, plane_imag, tables[2])
    plane_real, plane_imag = inner_step(plane_real, plane_imag, tables[3])
    return (plane_real, plane_imag)


def solution(mesh):
    placed = (P("outer", "inner", None, None), P("outer", "inner", None, None), P(), P(), P())
    return jax.shard_map(
        on_device,
        mesh=mesh,
        in_specs=placed,
        out_specs=(P("outer", "inner", None, None), P("outer", "inner", None, None)),
        check_vma=False,
    )
```

profile of v0, /device:TPU:33, one launch (start us, length us, event | category | flops | bytes accessed | tf_op | source)
XLA Modules:
  0.0 170.0 jit_solution(8441266659975682407)
XLA Ops:
  1.5 2.3 %fusion.20 = f32[512,512]{1,0:T(8,128)S(1)} fusion(f32[4,512,512]{2,1,0:T(8,128)} %param.8, s32[512]{0:T(512)S(1)} %bitcast.110), kind=kOutput, calls=%fused_computation.26 | convolution fusion | flops 1610874880 | bytes 2099200 | tf_op jit(solution)/shard_map/dot_general | solution.py:16
  3.8 2.3 %fusion.22 = f32[512,512]{1,0:T(8,128)S(1)} fusion(f32[4,512,512]{2,1,0:T(8,128)} %param.7, s32[512]{0:T(512)S(1)} %bitcast.111), kind=kOutput, calls=%fused_computation.28 | convolution fusion | flops 1610874880 | bytes 2099200 | tf_op jit(solution)/shard_map/dot_general | solution.py:13
  13.0 10.7 %all-to-all-start.1 = ((f32[1,1,256,512]{2,1,0,3:T(1,128)}), f32[1,1,256,512]{2,1,0,3:T(1,128)S(1)}, u32[]{:S(2)}, u32[]{:S(2)}) async-start(f32[1,1,256,512]{2,1,0,3:T(1,128)} %copy.10), calls=%async_computation.1 | async-start | bytes 1048576 | tf_op jit(solution)/shard_map/all_to_all | solution.py:49
  25.1 17.8 %all-to-all-done.1 = f32[1,1,256,512]{2,1,0,3:T(1,128)S(1)} async-done(((f32[1,1,256,512]{2,1,0,3:T(1,128)}), f32[1,1,256,512]{2,1,0,3:T(1,128)S(1)}, u32[]{:S(2)}, u32[]{:S(2)}) %all-to-all-start.1) | async-done | bytes 524320 | tf_op jit(solution)/shard_map/all_to_all | solution.py:49
  42.9 5.2 %all-to-all-start = ((f32[1,1,256,512]{2,1,0,3:T(1,128)}), f32[1,1,256,512]{2,1,0,3:T(1,128)}, u32[]{:S(2)}, u32[]{:S(2)}) async-start(f32[1,1,256,512]{2,1,0,3:T(1,128)} %copy.8), calls=%async_computation | async-start | bytes 1048576 | tf_op jit(solution)/shard_map/all_to_all | solution.py:48
  48.1 2.3 %fusion.16 = f32[512,512]{1,0:T(8,128)S(1)} fusion(f32[4,512,512]{2,1,0:T(8,128)} %param.8, s32[512]{0:T(512)S(1)} %bitcast.108), kind=kOutput, calls=%fused_computation.22 | convolution fusion | flops 1610874880 | bytes 2099200 | tf_op jit(solution)/shard_map/dot_general | solution.py:16
  50.4 2.3 %fusion.18 = f32[512,512]{1,0:T(8,128)S(1)} fusion(f32[4,512,512]{2,1,0:T(8,128)} %param.7, s32[512]{0:T(512)S(1)} %bitcast.109), kind=kOutput, calls=%fused_computation.24 | convolution fusion | flops 1610874880 | bytes 2099200 | tf_op jit(solution)/shard_map/dot_general | solution.py:13
  53.8 11.0 %all-to-all-done = f32[1,1,256,512]{2,1,0,3:T(1,128)} async-done(((f32[1,1,256,512]{2,1,0,3:T(1,128)}), f32[1,1,256,512]{2,1,0,3:T(1,128)}, u32[]{:S(2)}, u32[]{:S(2)}) %all-to-all-start) | async-done | bytes 524320 | tf_op jit(solution)/shard_map/all_to_all | solution.py:48
  66.9 3.1 %fusion.3 = f32[1,1,256,512]{3,2,1,0:T(8,128)} fusion(f32[256,512]{1,0:T(8,128)S(1)} %fusion.46, f32[256,512]{1,0:T(8,128)S(1)} %fusion.49, f32[512,512]{1,0:T(8,128)S(1)} %fusion.18, f32[512,512]{1,0:T(8,128)S(1)} %fusion.16, f32[1,1,256,512]{2,1,0,3:T(1,128)} %copy-done.2, f32[1,1,256,512]{2,1,0,3:T(1,128)} %all-to-all-done), kind=kOutput, calls=%fused_computation.7 | convolution fusion | flops 805961728 | bytes 4718592 | tf_op jit(solution)/shard_map/dot_general | solution.py:34
  72.0 5.8 %all-to-all-start.3 = ((f32[1,1,256,512]{2,1,0,3:T(1,128)}), f32[1,1,256,512]{2,1,0,3:T(1,128)S(1)}, u32[]{:S(2)}, u32[]{:S(2)}) async-start(f32[1,1,256,512]{2,1,0,3:T(1,128)} %copy.12), calls=%async_computation.3 | async-start | bytes 1048576 | tf_op jit(solution)/shard_map/all_to_all | solution.py:57
  78.9 12.9 %all-to-all-done.3 = f32[1,1,256,512]{2,1,0,3:T(1,128)S(1)} async-done(((f32[1,1,256,512]{2,1,0,3:T(1,128)}), f32[1,1,256,512]{2,1,0,3:T(1,128)S(1)}, u32[]{:S(2)}, u32[]{:S(2)}) %all-to-all-start.3) | async-done | bytes 524320 | tf_op jit(solution)/shard_map/all_to_all | solution.py:57
  91.8 5.1 %all-to-all-start.2 = ((f32[1,1,256,512]{2,1,0,3:T(1,128)}), f32[1,1,256,512]{2,1,0,3:T(1,128)}, u32[]{:S(2)}, u32[]{:S(2)}) async-start(f32[1,1,256,512]{2,1,0,3:T(1,128)} %copy.11), calls=%async_computation.2 | async-start | bytes 1048576 | tf_op jit(solution)/shard_map/all_to_all | solution.py:56
  96.9 2.4 %fusion.12 = f32[512,512]{1,0:T(8,128)S(1)} fusion(f32[4,512,512]{2,1,0:T(8,128)} %param.8, s32[512]{0:T(512)S(1)} %bitcast.106), kind=kOutput, calls=%fused_computation.18 | convolution fusion | flops 1610874880 | bytes 2099200 | tf_op jit(solution)/shard_map/dot_general | solution.py:16
  99.3 2.3 %fusion.14 = f32[512,512]{1,0:T(8,128)S(1)} fusion(f32[4,512,512]{2,1,0:T(8,128)} %param.7, s32[512]{0:T(512)S(1)} %bitcast.107), kind=kOutput, calls=%fused_computation.20 | convolution fusion | flops 1610874880 | bytes 2099200 | tf_op jit(solution)/shard_map/dot_general | solution.py:13
  102.7 7.9 %all-to-all-done.2 = f32[1,1,256,512]{2,1,0,3:T(1,128)} async-done(((f32[1,1,256,512]{2,1,0,3:T(1,128)}), f32[1,1,256,512]{2,1,0,3:T(1,128)}, u32[]{:S(2)}, u32[]{:S(2)}) %all-to-all-start.2) | async-done | bytes 524320 | tf_op jit(solution)/shard_map/all_to_all | solution.py:56
  110.6 2.1 %fusion.44 = f32[256,512]{1,0:T(8,128)S(1)} fusion(f32[512,512]{1,0:T(8,128)S(1)} %fusion.14, f32[1,1,256,512]{2,1,0,3:T(1,128)} %all-to-all-done.2), kind=kOutput, calls=%fused_computation.56 | convolution fusion | flops 805306368 | bytes 2097152 | tf_op jit(solution)/shard_map/dot_general | solution.py:28
  112.7 3.1 %fusion.5 = f32[1,1,256,512]{3,2,1,0:T(8,128)} fusion(f32[256,512]{1,0:T(8,128)S(1)} %fusion.41, f32[256,512]{1,0:T(8,128)S(1)} %fusion.44, f32[512,512]{1,0:T(8,128)S(1)} %fusion.14, f32[512,512]{1,0:T(8,128)S(1)} %fusion.12, f32[1,1,256,512]{2,1,0,3:T(1,128)} %copy-done.3, f32[1,1,256,512]{2,1,0,3:T(1,128)} %all-to-all-done.2), kind=kOutput, calls=%fused_computation.9 | convolution fusion | flops 805961728 | bytes 4718592 | tf_op jit(solution)/shard_map/dot_general | solution.py:34
  117.8 5.8 %all-to-all-start.5 = ((f32[1,1,256,512]{2,1,0,3:T(1,128)}), f32[1,1,256,512]{2,1,0,3:T(1,128)S(1)}, u32[]{:S(2)}, u32[]{:S(2)}) async-start(f32[1,1,256,512]{2,1,0,3:T(1,128)} %copy.14), calls=%async_computation.5 | async-start | bytes 1048576 | tf_op jit(solution)/shard_map/all_to_all | solution.py:49
  124.7 18.2 %all-to-all-done.5 = f32[1,1,256,512]{2,1,0,3:T(1,128)S(1)} async-done(((f32[1,1,256,512]{2,1,0,3:T(1,128)}), f32[1,1,256,512]{2,1,0,3:T(1,128)S(1)}, u32[]{:S(2)}, u32[]{:S(2)}) %all-to-all-start.5) | async-done | bytes 524320 | tf_op jit(solution)/shard_map/all_to_all | solution.py:49
  142.9 5.2 %all-to-all-start.4 = ((f32[1,1,256,512]{2,1,0,3:T(1,128)}), f32[1,1,256,512]{2,1,0,3:T(1,128)}, u32[]{:S(2)}, u32[]{:S(2)}) async-start(f32[1,1,256,512]{2,1,0,3:T(1,128)} %copy.13), calls=%async_computation.4 | async-start | bytes 1048576 | tf_op jit(solution)/shard_map/all_to_all | solution.py:48
  148.1 2.4 %fusion.8 = f32[512,512]{1,0:T(8,128)S(1)} fusion(f32[4,512,512]{2,1,0:T(8,128)} %param.8, s32[512]{0:T(512)S(1)} %bitcast.104), kind=kOutput, calls=%fused_computation.14 | convolution fusion | flops 1610874880 | bytes 2099200 | tf_op jit(solution)/shard_map/dot_general | solution.py:16
  150.5 2.3 %fusion.10 = f32[512,512]{1,0:T(8,128)S(1)} fusion(f32[4,512,512]{2,1,0:T(8,128)} %param.7, s32[512]{0:T(512)S(1)} %bitcast.105), kind=kOutput, calls=%fused_computation.16 | convolution fusion | flops 1610874880 | bytes 2099200 | tf_op jit(solution)/shard_map/dot_general | solution.py:13
  153.9 10.2 %all-to-all-done.4 = f32[1,1,256,512]{2,1,0,3:T(1,128)} async-done(((f32[1,1,256,512]{2,1,0,3:T(1,128)}), f32[1,1,256,512]{2,1,0,3:T(1,128)}, u32[]{:S(2)}, u32[]{:S(2)}) %all-to-all-start.4) | async-done | bytes 524320 | tf_op jit(solution)/shard_map/all_to_all | solution.py:48
  167.1 3.0 %fusion.7 = f32[1,1,256,512]{3,2,1,0:T(8,128)} fusion(f32[256,512]{1,0:T(8,128)S(1)} %fusion.36, f32[256,512]{1,0:T(8,128)S(1)} %fusion.39, f32[512,512]{1,0:T(8,128)S(1)} %fusion.10, f32[512,512]{1,0:T(8,128)S(1)} %fusion.8, f32[1,1,256,512]{2,1,0,3:T(1,128)S(1)} %copy-done.1, f32[1,1,256,512]{2,1,0,3:T(1,128)} %all-to-all-done.4), kind=kOutput, calls=%fused_computation.11 | convolution fusion | flops 805961728 | bytes 4718592 | tf_op jit(solution)/shard_map/dot_general | solution.py:34
  (33 shorter events, 23.4 us)
Async XLA Ops:
  0.6 5.5 %copy-start.6 = (f32[1,1,256,512]{3,2,1,0:T(8,128)S(1)}, f32[1,1,256,512]{3,2,1,0:T(8,128)}, u32[]{:S(2)}) copy-start(f32[1,1,256,512]{3,2,1,0:T(8,128)} %param.6) | copy-start | bytes 1572868
  0.6 7.3 %copy-start.5 = (f32[1,1,256,512]{3,2,1,0:T(8,128)S(1)}, f32[1,1,256,512]{3,2,1,0:T(8,128)}, u32[]{:S(2)}) copy-start(f32[1,1,256,512]{3,2,1,0:T(8,128)} %param.5) | copy-start | bytes 1572868
  13.0 29.9 %all-to-all-start.1 = ((f32[1,1,256,512]{2,1,0,3:T(1,128)}), f32[1,1,256,512]{2,1,0,3:T(1,128)S(1)}, u32[]{:S(2)}, u32[]{:S(2)}) async-start(f32[1,1,256,512]{2,1,0,3:T(1,128)} %copy.10), calls=%async_computation.1 | async-start | bytes 1048576 | tf_op jit(solution)/shard_map/all_to_all | solution.py:49
  42.9 10.9 %copy-start.2 = (f32[1,1,256,512]{2,1,0,3:T(1,128)}, f32[1,1,256,512]{2,1,0,3:T(1,128)S(1)}, u32[]{:S(2)}) copy-start(f32[1,1,256,512]{2,1,0,3:T(1,128)S(1)} %all-to-all-done.1) | copy-start | bytes 1572868
  42.9 22.0 %all-to-all-start = ((f32[1,1,256,512]{2,1,0,3:T(1,128)}), f32[1,1,256,512]{2,1,0,3:T(1,128)}, u32[]{:S(2)}, u32[]{:S(2)}) async-start(f32[1,1,256,512]{2,1,0,3:T(1,128)} %copy.8), calls=%async_computation | async-start | bytes 1048576 | tf_op jit(solution)/shard_map/all_to_all | solution.py:48
  72.0 19.8 %all-to-all-start.3 = ((f32[1,1,256,512]{2,1,0,3:T(1,128)}), f32[1,1,256,512]{2,1,0,3:T(1,128)S(1)}, u32[]{:S(2)}, u32[]{:S(2)}) async-start(f32[1,1,256,512]{2,1,0,3:T(1,128)} %copy.12), calls=%async_computation.3 | async-start | bytes 1048576 | tf_op jit(solution)/shard_map/all_to_all | solution.py:57
  91.8 5.1 %copy-start.3 = (f32[1,1,256,512]{2,1,0,3:T(1,128)}, f32[1,1,256,512]{2,1,0,3:T(1,128)S(1)}, u32[]{:S(2)}) copy-start(f32[1,1,256,512]{2,1,0,3:T(1,128)S(1)} %all-to-all-done.3) | copy-start | bytes 1572868
  91.8 18.8 %all-to-all-start.2 = ((f32[1,1,256,512]{2,1,0,3:T(1,128)}), f32[1,1,256,512]{2,1,0,3:T(1,128)}, u32[]{:S(2)}, u32[]{:S(2)}) async-start(f32[1,1,256,512]{2,1,0,3:T(1,128)} %copy.11), calls=%async_computation.2 | async-start | bytes 1048576 | tf_op jit(solution)/shard_map/all_to_all | solution.py:56
  96.9 4.7 %copy-start.4 = (f32[1,1,256,512]{2,1,0,3:T(1,128)S(1)}, f32[1,1,256,512]{2,1,0,3:T(1,128)}, u32[]{:S(2)}) copy-start(f32[1,1,256,512]{2,1,0,3:T(1,128)} %copy-done.3) | copy-start | bytes 1572868
  117.8 25.1 %all-to-all-start.5 = ((f32[1,1,256,512]{2,1,0,3:T(1,128)}), f32[1,1,256,512]{2,1,0,3:T(1,128)S(1)}, u32[]{:S(2)}, u32[]{:S(2)}) async-start(f32[1,1,256,512]{2,1,0,3:T(1,128)} %copy.14), calls=%async_computation.5 | async-start | bytes 1048576 | tf_op jit(solution)/shard_map/all_to_all | solution.py:49
  142.9 5.2 %copy-start = (f32[1,1,256,512]{2,1,0,3:T(1,128)}, f32[1,1,256,512]{2,1,0,3:T(1,128)S(1)}, u32[]{:S(2)}) copy-start(f32[1,1,256,512]{2,1,0,3:T(1,128)S(1)} %all-to-all-done.5) | copy-start | bytes 1572868
  142.9 21.2 %all-to-all-start.4 = ((f32[1,1,256,512]{2,1,0,3:T(1,128)}), f32[1,1,256,512]{2,1,0,3:T(1,128)}, u32[]{:S(2)}, u32[]{:S(2)}) async-start(f32[1,1,256,512]{2,1,0,3:T(1,128)} %copy.13), calls=%async_computation.4 | async-start | bytes 1048576 | tf_op jit(solution)/shard_map/all_to_all | solution.py:48
  148.1 4.7 %copy-start.1 = (f32[1,1,256,512]{2,1,0,3:T(1,128)S(1)}, f32[1,1,256,512]{2,1,0,3:T(1,128)}, u32[]{:S(2)}) copy-start(f32[1,1,256,512]{2,1,0,3:T(1,128)} %copy-done) | copy-start | bytes 1572868
where the time goes:
time: 171 us; the launch traced here: 170 us
  waiting for transfers between devices  78 us (46%)
  matrix products  42.7 us (25%)
  starting transfers between devices  37.9 us (22%)
  local copies, waits for them, and re-layouts  9.5 us (6%)
    all_to_all x2, waiting for transfers between devices, inner_step(): lax.all_to_all(plane_imag, 'inner', split_axis=3, concat_axis=3, tiled=True)  36 us
    all_to_all x2, waiting for transfers between devices, inner_step(): lax.all_to_all(plane_real, 'inner', split_axis=3, concat_axis=3, tiled=True)  21.2 us
    all_to_all x2, starting transfers between devices, inner_step(): lax.all_to_all(plane_imag, 'inner', split_axis=3, concat_axis=3, tiled=True)  16.5 us
    all_to_all x1, waiting for transfers between devices, outer_step(): lax.all_to_all(plane_imag, 'outer', split_axis=3, concat_axis=3, tiled=True)  12.9 us
    dot_general x4, matrix products, product(): jnp.dot(left_real + left_imag, moved_sum, precision=lax.Precision.HIGHEST...  11 us
    all_to_all x2, starting transfers between devices, inner_step(): lax.all_to_all(plane_real, 'inner', split_axis=3, concat_axis=3, tiled=True)  10.5 us
    dot_general x4, matrix products, prepare(): jnp.dot(selector, branch_imag, precision=lax.Precision.HIGHEST, preferred...  9.35 us
    dot_general x4, matrix products, prepare(): jnp.dot(selector, branch_real, precision=lax.Precision.HIGHEST, preferred...  9.24 us
  transfers between devices with their start and end apart: 6, of which 6 were waited for; matrix products, arithmetic and copies ran while one was open for 12% of the time, Pallas kernels for 0%

commit v1 on v0

--- a/solution.py
+++ b/solution.py
@@ -2,8 +2,19 @@
 import jax.numpy as jnp
 from jax import lax
 from jax.sharding import PartitionSpec as P
+from jax.lax import all_to_all, axis_size
 
 PRODUCTS = 4
+
+
+def sectors_group(across, block_in):
+    out_arr = all_to_all(
+        jnp.stack(jnp.split(block_in, axis_size(across), axis=3)),
+        split_axis=0,
+        axis_name=across,
+        concat_axis=0,
+    )
+    return jnp.concatenate(out_arr, axis=3)
 
 
 def prepare(branch_real, branch_imag, order):
@@ -45,7 +56,7 @@
 
 def inner_step(plane_real, plane_imag, prepared):
     return product(
-        lax.all_to_all(plane_real, "inner", split_axis=3, concat_axis=3, tiled=True),
+        sectors_group("inner", plane_real),
         lax.all_to_all(plane_imag, "inner", split_axis=3, concat_axis=3, tiled=True),
         prepared,
     )

time: 171 us -> 217 us (1.27)
  local copies, waits for them, and re-layouts: 9.5 us -> 60.5 us
  waiting for transfers between devices: 78 us -> 69.4 us
    unnamed x14 -> x36, local copies, waits for them, and re-layouts: 0.03 us -> 29.1 us
    another operation x0 -> x19, local copies, waits for them, and re-layouts: none -> 24.3 us  [sectors_group(): jnp.stack(jnp.split(block_in, axis_size(across), axis=3))]
    all_to_all x2, waiting for transfers between devices: 36 us -> 19.3 us  [inner_step(): lax.all_to_all(plane_imag, 'inner', split_axis=3, concat_axis=3, tiled=True)]
    all_to_all x2, waiting for transfers between devices: 21.2 us -> 29.2 us  [sectors_group(): all_to_all(jnp.stack(jnp.split(block_in, axis_size(across), axis=3)), spl...]
    all_to_all x2, starting transfers between devices: 10.5 us -> 17.1 us  [sectors_group(): all_to_all(jnp.stack(jnp.split(block_in, axis_size(across), axis=3)), spl...]
    all_to_all x2, starting transfers between devices: 16.5 us -> 9.86 us  [inner_step(): lax.all_to_all(plane_imag, 'inner', split_axis=3, concat_axis=3, tiled=True)]
    reshape x3 -> x1, local copies, waits for them, and re-layouts: 3.41 us -> 1.04 us  [product(): (first - second).reshape(1, 1, count, width)]
  transfers between devices with their start and end apart: 6 -> 6, of which waited for: 6 -> 6; matrix products, arithmetic and copies ran while one was open for 12% -> 14% of each run, Pallas kernels for 0% -> 0%
where the time goes in v1:
time: 217 us; the launch traced here: 215 us
  waiting for transfers between devices  69.4 us (32%)
  local copies, waits for them, and re-layouts  60.5 us (28%)
  matrix products  44.8 us (21%)
  starting transfers between devices  37.9 us (17%)
    all_to_all x2, waiting for transfers between devices, sectors_group(): all_to_all(jnp.stack(jnp.split(block_in, axis_size(across), axis=3)), spl...  29.2 us
    unnamed x36, local copies, waits for them, and re-layouts  29.1 us
    another operation x19, local copies, waits for them, and re-layouts, sectors_group(): jnp.stack(jnp.split(block_in, axis_size(across), axis=3))  24.3 us
    all_to_all x2, waiting for transfers between devices, inner_step(): lax.all_to_all(plane_imag, 'inner', split_axis=3, concat_axis=3, tiled=True)  19.3 us
    all_to_all x2, starting transfers between devices, sectors_group(): all_to_all(jnp.stack(jnp.split(block_in, axis_size(across), axis=3)), spl...  17.1 us
    all_to_all x1, waiting for transfers between devices, outer_step(): lax.all_to_all(plane_imag, 'outer', split_axis=3, concat_axis=3, tiled=True)  12.9 us
    dot_general x4, matrix products, product(): jnp.dot(left_real + left_imag, moved_sum, precision=lax.Precision.HIGHEST...  12.2 us
    all_to_all x2, starting transfers between devices, inner_step(): lax.all_to_all(plane_imag, 'inner', split_axis=3, concat_axis=3, tiled=True)  9.86 us
  transfers between devices with their start and end apart: 6, of which 6 were waited for; matrix products, arithmetic and copies ran while one was open for 14% of the time, Pallas kernels for 0%

profile of v1, /device:TPU:33, one launch (start us, length us, event | category | flops | bytes accessed | tf_op | source)
XLA Modules:
  0.0 214.6 jit_solution(7736206687082433146)
XLA Ops:
  1.5 2.3 %fusion.20 = f32[512,512]{1,0:T(8,128)S(1)} fusion(f32[4,512,512]{2,1,0:T(8,128)} %param.8, s32[512]{0:T(512)S(1)} %bitcast.202), kind=kOutput, calls=%fused_computation.26 | convolution fusion | flops 1610874880 | bytes 2099200 | tf_op jit(solution)/shard_map/dot_general | solution.py:27
  3.8 2.3 %fusion.22 = f32[512,512]{1,0:T(8,128)S(1)} fusion(f32[4,512,512]{2,1,0:T(8,128)} %param.7, s32[512]{0:T(512)S(1)} %bitcast.203), kind=kOutput, calls=%fused_computation.28 | convolution fusion | flops 1610874880 | bytes 2099200 | tf_op jit(solution)/shard_map/dot_general | solution.py:24
  19.7 10.7 %all-to-all-start = ((f32[16,1,1,256,32]{3,4,2,1,0:T(8,128)}), f32[16,1,1,256,32]{3,4,2,1,0:T(8,128)}, u32[]{:S(2)}, u32[]{:S(2)}) async-start(f32[16,1,1,256,32]{3,4,2,1,0:T(8,128)} %constant_dynamic-update-slice_fusion), calls=%async_computation | async-start | bytes 1048576 | tf_op jit(solution)/shard_map/all_to_all | solution.py:11
  30.5 3.0 %fusion.1 = f32[1,1,256,512]{2,3,1,0:T(8,128)S(1)} fusion(f32[256,512]{0,1:T(8,128)S(1)} %convolution_bitcast_fusion, f32[256,512]{0,1:T(8,128)S(1)} %convolution_bitcast_fusion.1, f32[512,512]{1,0:T(8,128)S(1)} %fusion.22, f32[512,512]{1,0:T(8,128)S(1)} %fusion.20, f32[1,1,256,512]{3,2,1,0:T(8,128)} %param.6, f32[1,1,256,512]{3,2,1,0:T(8,128)} %param.5), kind=kOutput, calls=%fused_computation.5 | convolution fusion | flops 805961728 | bytes 4718592 | tf_op jit(solution)/shard_map/dot_general | solution.py:45
  34.8 14.9 %all-to-all-done = f32[16,1,1,256,32]{3,4,2,1,0:T(8,128)} async-done(((f32[16,1,1,256,32]{3,4,2,1,0:T(8,128)}), f32[16,1,1,256,32]{3,4,2,1,0:T(8,128)}, u32[]{:S(2)}, u32[]{:S(2)}) %all-to-all-start) | async-done | bytes 524320 | tf_op jit(solution)/shard_map/all_to_all | solution.py:11
  49.8 5.2 %all-to-all-start.1 = ((f32[1,1,256,512]{2,1,0,3:T(1,128)}), f32[1,1,256,512]{2,1,0,3:T(1,128)}, u32[]{:S(2)}, u32[]{:S(2)}) async-start(f32[1,1,256,512]{2,1,0,3:T(1,128)} %copy.13), calls=%async_computation.1 | async-start | bytes 1048576 | tf_op jit(solution)/shard_map/all_to_all | solution.py:60
  55.0 2.3 %fusion.18 = f32[512,512]{1,0:T(8,128)S(1)} fusion(f32[4,512,512]{2,1,0:T(8,128)} %param.7, s32[512]{0:T(512)S(1)} %bitcast.200), kind=kOutput, calls=%fused_computation.24 | convolution fusion | flops 1610874880 | bytes 2099200 | tf_op jit(solution)/shard_map/dot_general | solution.py:24
  57.3 2.3 %fusion.16 = f32[512,512]{1,0:T(8,128)S(1)} fusion(f32[4,512,512]{2,1,0:T(8,128)} %param.8, s32[512]{0:T(512)S(1)} %bitcast.201), kind=kOutput, calls=%fused_computation.22 | convolution fusion | flops 1610874880 | bytes 2099200 | tf_op jit(solution)/shard_map/dot_general | solution.py:27
  61.7 10.0 %all-to-all-done.1 = f32[1,1,256,512]{2,1,0,3:T(1,128)} async-done(((f32[1,1,256,512]{2,1,0,3:T(1,128)}), f32[1,1,256,512]{2,1,0,3:T(1,128)}, u32[]{:S(2)}, u32[]{:S(2)}) %all-to-all-start.1) | async-done | bytes 524320 | tf_op jit(solution)/shard_map/all_to_all | solution.py:60
  73.8 3.1 %fusion.3 = f32[1,1,256,512]{3,2,1,0:T(8,128)} fusion(f32[256,512]{1,0:T(8,128)S(1)} %fusion.43, f32[256,512]{1,0:T(8,128)S(1)} %fusion.65, f32[512,512]{1,0:T(8,128)S(1)} %fusion.18, f32[512,512]{1,0:T(8,128)S(1)} %fusion.16, f32[256,512]{0,1:T(8,128)} %bitcast.25, f32[1,1,256,512]{2,1,0,3:T(1,128)} %all-to-all-done.1), kind=kOutput, calls=%fused_computation.7 | convolution fusion | flops 805961728 | bytes 4718592 | tf_op jit(solution)/shard_map/dot_general | solution.py:45
  78.9 5.8 %all-to-all-start.3 = ((f32[1,1,256,512]{2,1,0,3:T(1,128)}), f32[1,1,256,512]{2,1,0,3:T(1,128)S(1)}, u32[]{:S(2)}, u32[]{:S(2)}) async-start(f32[1,1,256,512]{2,1,0,3:T(1,128)} %copy.15), calls=%async_computation.3 | async-start | bytes 1048576 | tf_op jit(solution)/shard_map/all_to_all | solution.py:68
  85.8 12.9 %all-to-all-done.3 = f32[1,1,256,512]{2,1,0,3:T(1,128)S(1)} async-done(((f32[1,1,256,512]{2,1,0,3:T(1,128)}), f32[1,1,256,512]{2,1,0,3:T(1,128)S(1)}, u32[]{:S(2)}, u32[]{:S(2)}) %all-to-all-start.3) | async-done | bytes 524320 | tf_op jit(solution)/shard_map/all_to_all | solution.py:68
  98.7 5.1 %all-to-all-start.2 = ((f32[1,1,256,512]{2,1,0,3:T(1,128)}), f32[1,1,256,512]{2,1,0,3:T(1,128)}, u32[]{:S(2)}, u32[]{:S(2)}) async-start(f32[1,1,256,512]{2,1,0,3:T(1,128)} %copy.14), calls=%async_computation.2 | async-start | bytes 1048576 | tf_op jit(solution)/shard_map/all_to_all | solution.py:67
  103.8 2.3 %fusion.12 = f32[512,512]{1,0:T(8,128)S(1)} fusion(f32[4,512,512]{2,1,0:T(8,128)} %param.8, s32[512]{0:T(512)S(1)} %bitcast.198), kind=kOutput, calls=%fused_computation.18 | convolution fusion | flops 1610874880 | bytes 2099200 | tf_op jit(solution)/shard_map/dot_general | solution.py:27
  106.1 2.3 %fusion.14 = f32[512,512]{1,0:T(8,128)S(1)} fusion(f32[4,512,512]{2,1,0:T(8,128)} %param.7, s32[512]{0:T(512)S(1)} %bitcast.199), kind=kOutput, calls=%fused_computation.20 | convolution fusion | flops 1610874880 | bytes 2099200 | tf_op jit(solution)/shard_map/dot_general | solution.py:24
  109.5 8.0 %all-to-all-done.2 = f32[1,1,256,512]{2,1,0,3:T(1,128)} async-done(((f32[1,1,256,512]{2,1,0,3:T(1,128)}), f32[1,1,256,512]{2,1,0,3:T(1,128)}, u32[]{:S(2)}, u32[]{:S(2)}) %all-to-all-start.2) | async-done | bytes 524320 | tf_op jit(solution)/shard_map/all_to_all | solution.py:67
  163.3 6.4 %all-to-all-start.4 = ((f32[16,1,1,256,32]{3,4,2,1,0:T(8,128)}), f32[16,1,1,256,32]{3,4,2,1,0:T(8,128)}, u32[]{:S(2)}, u32[]{:S(2)}) async-start(f32[16,1,1,256,32]{3,4,2,1,0:T(8,128)} %constant_dynamic-update-slice_fusion.16), calls=%async_computation.4 | async-start | bytes 1048576 | tf_op jit(solution)/shard_map/all_to_all | solution.py:11
  169.7 3.1 %fusion.5 = f32[1,1,256,512]{3,2,1,0:T(8,128)} fusion(f32[256,512]{1,0:T(8,128)S(1)} %fusion.38, f32[256,512]{1,0:T(8,128)S(1)} %fusion.41, f32[512,512]{1,0:T(8,128)S(1)} %fusion.14, f32[512,512]{1,0:T(8,128)S(1)} %fusion.12, f32[1,1,256,512]{2,1,0,3:T(1,128)} %copy-done, f32[1,1,256,512]{2,1,0,3:T(1,128)} %all-to-all-done.2), kind=kOutput, calls=%fused_computation.9 | convolution fusion | flops 805961728 | bytes 4718592 | tf_op jit(solution)/shard_map/dot_general | solution.py:45
  174.8 14.3 %all-to-all-done.4 = f32[16,1,1,256,32]{3,4,2,1,0:T(8,128)} async-done(((f32[16,1,1,256,32]{3,4,2,1,0:T(8,128)}), f32[16,1,1,256,32]{3,4,2,1,0:T(8,128)}, u32[]{:S(2)}, u32[]{:S(2)}) %all-to-all-start.4) | async-done | bytes 524320 | tf_op jit(solution)/shard_map/all_to_all | solution.py:11
  189.1 4.6 %all-to-all-start.5 = ((f32[1,1,256,512]{2,1,0,3:T(1,128)}), f32[1,1,256,512]{2,1,0,3:T(1,128)S(1)}, u32[]{:S(2)}, u32[]{:S(2)}) async-start(f32[1,1,256,512]{2,1,0,3:T(1,128)} %copy.33), calls=%async_computation.5 | async-start | bytes 1048576 | tf_op jit(solution)/shard_map/all_to_all | solution.py:60
  193.7 2.3 %fusion.8 = f32[512,512]{1,0:T(8,128)S(1)} fusion(f32[4,512,512]{2,1,0:T(8,128)} %param.8, s32[512]{0:T(512)S(1)} %bitcast.196), kind=kOutput, calls=%fused_computation.14 | convolution fusion | flops 1610874880 | bytes 2099200 | tf_op jit(solution)/shard_map/dot_general | solution.py:27
  196.0 2.3 %fusion.10 = f32[512,512]{1,0:T(8,128)S(1)} fusion(f32[4,512,512]{2,1,0:T(8,128)} %param.7, s32[512]{0:T(512)S(1)} %bitcast.197), kind=kOutput, calls=%fused_computation.16 | convolution fusion | flops 1610874880 | bytes 2099200 | tf_op jit(solution)/shard_map/dot_general | solution.py:24
  200.4 9.3 %all-to-all-done.5 = f32[1,1,256,512]{2,1,0,3:T(1,128)S(1)} async-done(((f32[1,1,256,512]{2,1,0,3:T(1,128)}), f32[1,1,256,512]{2,1,0,3:T(1,128)S(1)}, u32[]{:S(2)}, u32[]{:S(2)}) %all-to-all-start.5) | async-done | bytes 524320 | tf_op jit(solution)/shard_map/all_to_all | solution.py:60
  211.7 3.0 %fusion.7 = f32[1,1,256,512]{3,2,1,0:T(8,128)} fusion(f32[256,512]{1,0:T(8,128)S(1)} %fusion.36, f32[256,512]{1,0:T(8,128)S(1)} %fusion.66, f32[512,512]{1,0:T(8,128)S(1)} %fusion.10, f32[512,512]{1,0:T(8,128)S(1)} %fusion.8, f32[256,512]{0,1:T(8,128)} %bitcast.55, f32[1,1,256,512]{2,1,0,3:T(1,128)S(1)} %all-to-all-done.5), kind=kOutput, calls=%fused_computation.11 | convolution fusion | flops 805961728 | bytes 4718592 | tf_op jit(solution)/shard_map/dot_general | solution.py:45
  (72 shorter events, 75.8 us)
Async XLA Ops:
  0.6 5.5 %copy-start.2 = (f32[1,1,256,512]{3,2,1,0:T(8,128)S(1)}, f32[1,1,256,512]{3,2,1,0:T(8,128)}, u32[]{:S(2)}) copy-start(f32[1,1,256,512]{3,2,1,0:T(8,128)} %param.6) | copy-start | bytes 1572868
  0.6 7.3 %copy-start.1 = (f32[1,1,256,512]{3,2,1,0:T(8,128)S(1)}, f32[1,1,256,512]{3,2,1,0:T(8,128)}, u32[]{:S(2)}) copy-start(f32[1,1,256,512]{3,2,1,0:T(8,128)} %param.5) | copy-start | bytes 1572868
  19.7 30.0 %all-to-all-start = ((f32[16,1,1,256,32]{3,4,2,1,0:T(8,128)}), f32[16,1,1,256,32]{3,4,2,1,0:T(8,128)}, u32[]{:S(2)}, u32[]{:S(2)}) async-start(f32[16,1,1,256,32]{3,4,2,1,0:T(8,128)} %constant_dynamic-update-slice_fusion), calls=%async_computation | async-start | bytes 1048576 | tf_op jit(solution)/shard_map/all_to_all | solution.py:11
  49.8 22.0 %all-to-all-start.1 = ((f32[1,1,256,512]{2,1,0,3:T(1,128)}), f32[1,1,256,512]{2,1,0,3:T(1,128)}, u32[]{:S(2)}, u32[]{:S(2)}) async-start(f32[1,1,256,512]{2,1,0,3:T(1,128)} %copy.13), calls=%async_computation.1 | async-start | bytes 1048576 | tf_op jit(solution)/shard_map/all_to_all | solution.py:60
  78.9 19.8 %all-to-all-start.3 = ((f32[1,1,256,512]{2,1,0,3:T(1,128)}), f32[1,1,256,512]{2,1,0,3:T(1,128)S(1)}, u32[]{:S(2)}, u32[]{:S(2)}) async-start(f32[1,1,256,512]{2,1,0,3:T(1,128)} %copy.15), calls=%async_computation.3 | async-start | bytes 1048576 | tf_op jit(solution)/shard_map/all_to_all | solution.py:68
  98.7 10.8 %copy-start = (f32[1,1,256,512]{2,1,0,3:T(1,128)}, f32[1,1,256,512]{2,1,0,3:T(1,128)S(1)}, u32[]{:S(2)}) copy-start(f32[1,1,256,512]{2,1,0,3:T(1,128)S(1)} %all-to-all-done.3) | copy-start | bytes 1572868
  98.7 18.8 %all-to-all-start.2 = ((f32[1,1,256,512]{2,1,0,3:T(1,128)}), f32[1,1,256,512]{2,1,0,3:T(1,128)}, u32[]{:S(2)}, u32[]{:S(2)}) async-start(f32[1,1,256,512]{2,1,0,3:T(1,128)} %copy.14), calls=%async_computation.2 | async-start | bytes 1048576 | tf_op jit(solution)/shard_map/all_to_all | solution.py:67
  163.3 25.8 %all-to-all-start.4 = ((f32[16,1,1,256,32]{3,4,2,1,0:T(8,128)}), f32[16,1,1,256,32]{3,4,2,1,0:T(8,128)}, u32[]{:S(2)}, u32[]{:S(2)}) async-start(f32[16,1,1,256,32]{3,4,2,1,0:T(8,128)} %constant_dynamic-update-slice_fusion.16), calls=%async_computation.4 | async-start | bytes 1048576 | tf_op jit(solution)/shard_map/all_to_all | solution.py:11
  189.1 20.7 %all-to-all-start.5 = ((f32[1,1,256,512]{2,1,0,3:T(1,128)}), f32[1,1,256,512]{2,1,0,3:T(1,128)S(1)}, u32[]{:S(2)}, u32[]{:S(2)}) async-start(f32[1,1,256,512]{2,1,0,3:T(1,128)} %copy.33), calls=%async_computation.5 | async-start | bytes 1048576 | tf_op jit(solution)/shard_map/all_to_all | solution.py:60
